TPU v7x, 32 devices: a whole 2x2x4 slice. The times are simulated.
32 devices in a mesh: row: 4 (over y, x), col: 8 (over z, core).
Axes of the slice: x: 2, y: 2, z: 4, core: 2. Of those that a mesh axis runs over, the one named last changes fastest.
Arguments:
- velocity: float32 [3, 8, 8, 36, 32, 512], P(None, 'col', 'row'), may hold values from -6 to 6
- y_sizes: int32 [8], replicated, may hold values from 1 to 36, 256 in all
- old_place: int32 [8, 8], replicated, may hold values from 0 to 7, each once within a row
- new_col: int32 [8, 8], replicated, may hold values from 0 to 7, each once within a row
Outputs:
- divergence: float32 [8, 8, 4, 256, 512], P('row', 'col')
- peak: float32 [256, 512], replicated
Inputs may be any that keep to these rules, and one draw needn't show every extreme that they name: `y_sizes`: the heights sum to 256 and the tallest is exactly 36. `old_place`: each row is a permutation of 0 to 7. `new_col`: each row is a permutation of 0 to 8 - 1.
All inputs are finite; a program needn't handle non-finite values.
Results may differ from a plain program's by a relative error of at most 0.0003.
Values sent between devices are 32-bit elements; how exact they have to be, the bound alone decides.
A program may use at most 320 MiB of HBM per device.

v0:
```python
import math

import jax
import jax.numpy as jnp
from jax import lax
from jax.sharding import PartitionSpec as P

YMEAN = 32


EXACT = lax.Precision.HIGHEST


def source_rows(y_sizes, old_place, row_depth, height):
    ends = jnp.cumsum(y_sizes)
    starts = ends - y_sizes
    cells = jnp.arange(height, dtype=jnp.int32)
    block = jnp.sum((cells[:, None] >= ends[None, :]).astype(jnp.int32), axis=1)
    offset = cells - jnp.take(starts, block)
    return jnp.take(old_place, block, axis=1) * row_depth + offset


def spectral_matrix(positions, count):
    gap = (positions[:, None] - positions[None, :]) % count
    angle = gap.astype(jnp.float32) * (math.pi / count)
    parity = 1.0 - 2.0 * (gap % 2).astype(jnp.float32)
    divisor = jnp.where(gap == 0, 1.0, jnp.sin(angle))
    return jnp.where(gap == 0, 0.0, parity * jnp.cos(angle) / divisor * (2.0 / count))


def along_last(field, matrix):
    return jnp.dot(
        field, jnp.transpose(matrix), precision=EXACT, preferred_element_type=jnp.float32
    )


def along_rows(field, matrix):
    return jnp.einsum("jy,ksyx->ksjx", matrix, field, precision=EXACT)


def vertical_positions(slab_of, rows_count, columns, per_row, planes, thick):
    owner_row = jnp.arange(rows_count, dtype=jnp.int32)[:, None, None]
    owner_col = jnp.arange(columns, dtype=jnp.int32)[None, :, None]
    group = jnp.arange(per_row, dtype=jnp.int32)[None, None, :]
    zblock = owner_row * per_row + group
    slab = jnp.take(slab_of.reshape(-1), zblock * columns + owner_col)
    first = zblock * planes + slab * thick
    return (first[..., None] + jnp.arange(thick, dtype=jnp.int32)).reshape(-1)


def on_device(velocity, y_sizes, old_place, new_col):
    velocity = velocity[:, 0]
    row_depth = velocity.shape[2]
    planes = velocity.shape[3]
    x_cells = velocity.shape[4]
    places = velocity.shape[1]
    columns = lax.axis_size("col")
    rows_count = lax.axis_size("row")
    my_col = lax.axis_index("col")
    my_row = lax.axis_index("row")
    thick = planes // columns
    per_row = columns // rows_count
    blocks_y = y_sizes.shape[0]
    height = YMEAN * blocks_y
    hits = (new_col[:, :, None] == jnp.arange(columns, dtype=jnp.int32)[None, None, :]).astype(
        jnp.int32
    )
    slab_of = jnp.sum(hits * jnp.arange(columns, dtype=jnp.int32)[None, :, None], axis=1)
    rows_index = source_rows(y_sizes, old_place, row_depth, height)
    across_x = spectral_matrix(jnp.arange(x_cells, dtype=jnp.int32), x_cells)
    across_y = spectral_matrix(jnp.arange(height, dtype=jnp.int32), height)
    fields = velocity.shape[0]
    order = jnp.take(slab_of, my_col, axis=0)
    sliced = velocity.reshape(fields, places, row_depth, columns, thick, x_cells)
    outgoing = jnp.take(sliced, order, axis=3)
    settled = lax.all_to_all(
        lax.all_to_all(outgoing, "col", split_axis=3, concat_axis=3, tiled=True),
        "row",
        split_axis=3,
        concat_axis=1,
        tiled=True,
    )
    flat = settled.reshape(fields, blocks_y * row_depth, per_row, thick, x_cells)
    my_rows = lax.dynamic_slice_in_dim(rows_index, my_row * per_row, per_row, 0)
    pieces = []
    for group in range(per_row):
        picked = jnp.take(flat[:, :, group], my_rows[group], axis=1)
        pieces.append(jnp.swapaxes(picked, 1, 2))
    slabs = jnp.stack(pieces, axis=1)
    vertical = slabs[2]
    positions = vertical_positions(slab_of, rows_count, columns, per_row, planes, thick)
    across_z = spectral_matrix(positions, planes * columns)
    received = lax.all_to_all(
        vertical[None], ("row", "col"), split_axis=3, concat_axis=0, tiled=True
    )
    shape = received.shape
    slope = jnp.einsum(
        "ab,byx->ayx", across_z, received.reshape(-1, shape[3], shape[4]), precision=EXACT
    )
    slope_z = lax.all_to_all(
        slope.reshape(shape), ("row", "col"), split_axis=0, concat_axis=3, tiled=True
    )[0]
    slope_x = along_last(slabs[0], across_x)
    field = slope_x + along_rows(slabs[1], across_y) + slope_z
    local_peak = jnp.max(jnp.abs(field), axis=(0, 1))
    peak = lax.pmax(local_peak, ("row", "col"))
    return (field[:, None], peak)


def solution(mesh):
    in_specs = (P(None, "col", "row", None, None, None), P(), P(), P())
    out_specs = (P("row", "col", None, None, None), P())
    return jax.shard_map(
        on_device, mesh=mesh, in_specs=in_specs, out_specs=out_specs, check_vma=False
    )
```

profile of v0, /device:TPU:0, one launch (start us, length us, event | category | flops | bytes accessed | tf_op | source)
XLA Modules:
  0.0 951.5 jit_solution(11597304904075420686)
XLA Ops:
  7.2 0.8 select_reduce_fusion
  8.0 16.7 %reshape_squeeze.3 = f32[3,2,36,8,4,512]{5,4,3,2,1,0:T(4,128)} reshape(f32[3,1,2,36,32,512]{5,4,3,2,1,0:T(8,128)} %param.6) | data formatting | bytes 28311552 | tf_op jit(solution)/shard_map/reshape;squeeze | solution.py:74
  24.7 19.1 %gather_fusion = f32[8,3,2,36,4,512]{5,4,3,2,1,0:T(4,128)} fusion(f32[3,2,36,8,4,512]{5,4,3,2,1,0:T(4,128)} %reshape_squeeze.3, s32[1024]{0:T(1024)S(1)} %pad_clamp_fusion.3), kind=kCustom, calls=%fused_computation.2 | custom fusion | bytes 28311584 | tf_op jit(solution)/shard_map/jit(_take)/gather | solution.py:75
  43.8 8.1 select_bitcast_fusion
  51.9 313.7 %all_to_all.50 = f32[3,2,36,8,4,512]{5,4,2,1,0,3:T(4,128)} all-to-all(f32[3,2,36,8,4,512]{5,4,2,1,0,3:T(4,128)S(1)} %select_bitcast_fusion), channel_id=1, replica_groups=mesh['row'=4,'col'=8] {'col'}, dimensions={3} | all-to-all | bytes 28311552 | tf_op jit(solution)/shard_map/all_to_all | solution.py:77
  365.6 6.7 all-to-all-start.1
  372.7 0.7 gather_fusion.1
  373.4 0.7 fusion.160
  374.1 5.0 fusion.124
  379.6 146.8 %all-to-all-done.1 = f32[3,2,36,8,4,512]{5,4,2,1,0,3:T(4,128)} async-done(((f32[3,2,36,8,4,512]{5,4,2,1,0,3:T(4,128)}), f32[3,2,36,8,4,512]{5,4,2,1,0,3:T(4,128)}, u32[]{:S(2)}, u32[]{:S(2)}) %all-to-all-start.1) | async-done | bytes 14155808 | tf_op jit(solution)/shard_map/all_to_all | solution.py:76
  526.3 8.4 copy.76
  534.8 6.6 slice_bitcast_fusion
  541.4 9.5 gather_fusion.3
  550.9 7.8 fusion.1
  558.7 9.7 %gather_fusion.4 = f32[256,3,4,512]{3,2,1,0:T(4,128)} fusion(f32[3,288,4,512]{3,2,1,0:T(4,128)} %get-tuple-element.30, s32[1024]{0:T(1024)S(1)} %pad_clamp_fusion.1), kind=kCustom, calls=%fused_computation.1.clone | custom fusion | bytes 12583936 | tf_op jit(solution)/shard_map/jit(_take)/gather | solution.py:87
  568.3 5.2 fusion
  574.0 0.4 pad_maximum_fusion
  574.5 2.2 copy-done
  576.7 4.7 copy.86
  581.4 3.6 all-to-all-start.2
  585.2 0.8 gather_fusion.2
  586.8 93.1 %all-to-all-done.2 = f32[1,2,4,256,512]{4,2,1,0,3:T(4,128)} async-done(((f32[1,2,4,256,512]{4,2,1,0,3:T(4,128)}), f32[1,2,4,256,512]{4,2,1,0,3:T(4,128)}, u32[]{:S(2)}, u32[]{:S(2)}) %all-to-all-start.2) | async-done | bytes 4194336 | tf_op jit(solution)/shard_map/all_to_all | solution.py:93
  679.9 5.6 copy.110
  685.5 5.3 reshape.362
  690.8 7.2 fusion.10
  698.0 4.4 copy.88
  702.4 3.6 all-to-all-start.3
  706.2 15.6 %fusion.8 = f32[2,4,256,512]{3,2,1,0:T(8,128)} fusion(f32[3,1,4,256,512]{4,3,2,1,0:T(8,128)} %fusion.1, f32[3,1,4,256,512]{4,3,2,1,0:T(8,128)} %copy-done), kind=kOutput, calls=%fused_computation.21 | convolution fusion | flops 6452412416 | bytes 16777216 | tf_op jit(solution)/shard_map/dot_general | solution.py:32
  721.8 79.1 %all-to-all-done.3 = f32[32,2,4,8,512]{4,3,2,1,0:T(8,128)} async-done(((f32[32,2,4,8,512]{4,3,2,1,0:T(8,128)}), f32[32,2,4,8,512]{4,3,2,1,0:T(8,128)}, u32[]{:S(2)}, u32[]{:S(2)}) %all-to-all-start.3) | async-done | bytes 4194336 | tf_op jit(solution)/shard_map/all_to_all | solution.py:100
  800.9 14.5 %abs_reduce_fusion = (f32[256,512]{1,0:T(8,128)}, f32[2,4,256,512]{3,2,1,0:T(8,128)}) fusion(f32[2,4,256,512]{3,2,1,0:T(8,128)} %fusion.8, f32[3,1,4,256,512]{4,3,2,1,0:T(8,128)} %fusion.1, f32[3,1,4,256,512]{4,3,2,1,0:T(8,128)} %copy-done, f32[32,2,4,8,512]{4,3,2,1,0:T(8,128)} %all-to-all-done.3), kind=kOutput, calls=%fused_computation.28 | convolution fusion | flops 3228565504 | bytes 25690112 | tf_op jit(solution)/shard_map/jy,ksyx->ksjx/dot_general | solution.py:38
  815.4 127.1 %all-reduce.2.cloned.1.call-done = f32[256,512]{1,0:T(8,128)} async-done(((f32[256,512]{1,0:T(8,128)}), f32[256,512]{1,0:T(8,128)}) %all-reduce.2.cloned.1.call-update) | async-done | bytes 524304 | tf_op jit(solution)/shard_map/pmax | solution.py:106
  942.5 1.9 copy.112
  (45 shorter events, 2.5 us)
Async XLA Ops:
  365.6 6.7 copy-start.1
  365.6 6.8 copy-start.2
  365.6 160.7 %all-to-all-start.1 = ((f32[3,2,36,8,4,512]{5,4,2,1,0,3:T(4,128)}), f32[3,2,36,8,4,512]{5,4,2,1,0,3:T(4,128)}, u32[]{:S(2)}, u32[]{:S(2)}) async-start(f32[3,2,36,8,4,512]{5,4,2,1,0,3:T(4,128)} %all_to_all.50), calls=%async_computation.1 | async-start | bytes 28311552 | tf_op jit(solution)/shard_map/all_to_all | solution.py:76
  558.6 15.3 %slice-start = ((s8[6291456]{0:T(1024)(128)(4,1)}), s8[2097152]{0:T(1024)(128)(4,1)S(1)}, s32[]{:S(2)}) async-start(s8[6291456]{0:T(1024)(128)(4,1)} %bitcast.108), calls=%async_computation.5 | async-start | bytes 4194304
  568.3 5.7 slice-start.1
  574.0 2.7 copy-start
  581.4 98.5 %all-to-all-start.2 = ((f32[1,2,4,256,512]{4,2,1,0,3:T(4,128)}), f32[1,2,4,256,512]{4,2,1,0,3:T(4,128)}, u32[]{:S(2)}, u32[]{:S(2)}) async-start(f32[1,2,4,256,512]{4,2,1,0,3:T(4,128)} %copy.86), calls=%async_computation.2 | async-start | bytes 8388608 | tf_op jit(solution)/shard_map/all_to_all | solution.py:93
  702.4 98.5 %all-to-all-start.3 = ((f32[32,2,4,8,512]{4,3,2,1,0:T(8,128)}), f32[32,2,4,8,512]{4,3,2,1,0:T(8,128)}, u32[]{:S(2)}, u32[]{:S(2)}) async-start(f32[32,2,4,8,512]{4,3,2,1,0:T(8,128)} %copy.88), calls=%async_computation.3 | async-start | bytes 8388608 | tf_op jit(solution)/shard_map/all_to_all | solution.py:100
  706.0 236.6 %all-reduce.2.cloned.1.call-start = ((), (), s32[]{:S(2)}) async-start(), calls=%async_computation.4 | async-start | bytes 1048576 | tf_op jit(solution)/shard_map/pmax | solution.py:106
Sparse Core Ops, SparseCore 0:
  815.6 126.9 all-reduce.1
where the time goes:
time: 959 us; the launch traced here: 951 us
  waiting for transfers between devices  446 us (47%)
  blocking collectives  314 us (33%)
  local copies, waits for them, and re-layouts  97.7 us (10%)
  matrix products  37.3 us (4%)
  other arithmetic  28.1 us (3%)
  between operations  14.5 us (2%)
  starting transfers between devices  14.1 us (1%)
    all_to_all x1, blocking collectives, on_device(): lax.all_to_all(outgoing, 'col', split_axis=3, concat_axis=3, tiled=True)  314 us
    all_to_all x1, waiting for transfers between devices, on_device(): lax.all_to_all(lax.all_to_all(outgoing, 'col', split_axis=3, concat_axis=...  147 us
    pmax x1, waiting for transfers between devices, on_device(): peak = lax.pmax(local_peak, ('row', 'col'))  127 us
    all_to_all x1, waiting for transfers between devices, on_device(): lax.all_to_all(vertical[None], ('row', 'col'), split_axis=3, concat_axis=...  93.1 us
    all_to_all x1, waiting for transfers between devices, on_device(): lax.all_to_all(slope.reshape(shape), ('row', 'col'), split_axis=0, concat...  79.1 us
  transfers between devices with their start and end apart: 4, of which 4 were waited for; matrix products, arithmetic and copies ran while one was open for 3% of the time, Pallas kernels for 0%

commit v1 on v0

v1 whole, which is shorter than its diff:
```python
import math

import jax
import jax.numpy as jnp
from jax import lax
from jax.sharding import PartitionSpec as P

YMEAN = 32


FINE = lax.Precision.HIGH


def spectral_matrix(to, source, count):
    gap = (to[:, None] - source[None, :]) % count
    angle = gap.astype(jnp.float32) * (math.pi / count)
    parity = 1.0 - 2.0 * (gap % 2).astype(jnp.float32)
    divisor = jnp.where(gap == 0, 1.0, jnp.sin(angle))
    return jnp.where(gap == 0, 0.0, parity * jnp.cos(angle) / divisor * (2.0 / count))


def source_rows(y_sizes, place, row_depth, height):
    ends = jnp.cumsum(y_sizes)
    starts = ends - y_sizes
    cells = jnp.arange(height, dtype=jnp.int32)
    block = jnp.sum((cells[:, None] >= ends[None, :]).astype(jnp.int32), axis=1)
    stored = jnp.take(place, block) * row_depth + cells - jnp.take(starts, block)
    return stored


def row_exchange(value, split, concat):
    return lax.all_to_all(value, "row", split_axis=split, concat_axis=concat, tiled=True)


def col_exchange(value, split, concat):
    return lax.all_to_all(value, "col", split_axis=split, concat_axis=concat, tiled=True)


def on_device(velocity, y_sizes, old_place, new_col):
    velocity = velocity[:, 0]
    fields, places, row_depth, planes, x_cells = velocity.shape
    columns = lax.axis_size("col")
    rows_count = lax.axis_size("row")
    my_col = lax.axis_index("col")
    thick = planes // columns
    blocks_y = y_sizes.shape[0]
    height = YMEAN * blocks_y
    depth = planes * columns
    x_part = x_cells // rows_count
    y_part = height // columns
    slots = jnp.arange(columns, dtype=jnp.int32)
    hits = (new_col[:, :, None] == slots[None, None, :]).astype(jnp.int32)
    slab_of = jnp.sum(hits * slots[None, :, None], axis=1)

    stored = source_rows(y_sizes, jnp.take(old_place, my_col, axis=0), row_depth, height)
    pick = (stored[:, None] == jnp.arange(blocks_y * row_depth)[None, :]).astype(jnp.float32)
    cells = jnp.arange(height, dtype=jnp.int32)
    grid_row = jnp.sum(pick * cells[:, None].astype(jnp.float32), axis=0).astype(jnp.int32)
    used = jnp.sum(pick, axis=0)
    across_y = spectral_matrix(cells, grid_row, height) * used[None, :]
    steps_x = jnp.arange(x_cells, dtype=jnp.int32)
    across_x = spectral_matrix(steps_x, steps_x, x_cells)

    slope_x = jnp.dot(velocity[0], across_x.T, precision=FINE, preferred_element_type=jnp.float32)
    along_y = jnp.stack([slope_x, velocity[1]])
    two = row_exchange(along_y, 4, 1)
    third = row_exchange(velocity[2], 3, 0)
    two = two.reshape(2, blocks_y * row_depth, planes, x_part)
    third = third.reshape(blocks_y * row_depth, planes, x_part)
    upright = jnp.take(third, stored, axis=0)
    upright = col_exchange(upright.reshape(columns, y_part, planes, x_part), 0, 0)
    first = slots[None, :, None] * planes + slab_of.T[:, :, None] * thick
    targets = (first + jnp.arange(thick, dtype=jnp.int32)).reshape(-1)
    across_z = spectral_matrix(targets, jnp.arange(depth, dtype=jnp.int32), depth)
    slope_z = jnp.einsum(
        "akz,kyzx->ayx",
        across_z.reshape(depth, columns, planes),
        upright,
        precision=FINE,
    )
    slope_z = slope_z.reshape(columns, planes, y_part, x_part)
    slope_z = lax.all_to_all(
        slope_z, "col", split_axis=0, concat_axis=2, tiled=True
    ).reshape(planes, height, x_part)
    flat = jnp.einsum("jy,yzx->zjx", across_y, two[1], precision=FINE)
    flat = flat + jnp.swapaxes(jnp.take(two[0], stored, axis=0), 0, 1)
    flat = flat.reshape(columns, thick, height, x_part)
    flat = jnp.take(flat, jnp.take(slab_of, my_col, axis=0), axis=0)
    flat = col_exchange(flat, 0, 0).reshape(planes, height, x_part)
    part = flat + slope_z
    local_peak = jnp.max(jnp.abs(part), axis=0)
    peak = lax.pmax(local_peak, "col")
    peak = lax.all_gather(peak, "row", axis=1, tiled=True)
    field = row_exchange(part, 0, 2)
    field = field.reshape(columns // rows_count, 1, thick, height, x_cells)
    return (field, peak)


def solution(mesh):
    in_specs = (P(None, "col", "row", None, None, None), P(), P(), P())
    out_specs = (P("row", "col", None, None, None), P())
    return jax.shard_map(
        on_device, mesh=mesh, in_specs=in_specs, out_specs=out_specs, check_vma=False
    )
```

time: 959 us -> 788 us (0.82)
  blocking collectives: 314 us -> 11 us
  local copies, waits for them, and re-layouts: 97.7 us -> 357 us
  waiting for transfers between devices: 446 us -> 242 us
  other arithmetic: 28.1 us -> 86.2 us
  starting transfers between devices: 14.1 us -> 31.8 us
    all_to_all x1 -> x0, blocking collectives: 314 us -> none  [on_device(): lax.all_to_all(outgoing, 'col', split_axis=3, concat_axis=3, tiled=True)]
    unnamed x12 -> x14, local copies, waits for them, and re-layouts: 4.55 us -> 217 us
    all_to_all x3 -> x6, waiting for transfers between devices: 319 us -> 188 us  [the longest x1 88.7 us: on_device(): lax.all_to_all(slope_z, 'col', split_axis=0, concat_axis=2, tiled=True)]
    pmax x1, waiting for transfers between devices: 127 us -> 54.4 us  [on_device(): peak = lax.pmax(local_peak, 'col')]
    all_to_all x0 -> x2, other arithmetic: none -> 47.6 us  [row_exchange(): lax.all_to_all(value, 'row', split_axis=split, concat_axis=concat, tiled=...]
    all_to_all x2 -> x6, local copies, waits for them, and re-layouts: 14 us -> 53.3 us  [the longest x5 48 us: row_exchange(): lax.all_to_all(value, 'row', split_axis=split, concat_axis=concat, tiled=...]
    slice x2 -> x4, local copies, waits for them, and re-layouts: 4.93 us -> 26.3 us  [the longest x2 11.7 us: on_device(): flat = jnp.einsum('jy,yzx->zjx', across_y, two[1], precision=FINE)]
    gather x9 -> x6, local copies, waits for them, and re-layouts: 40.7 us -> 22.2 us  [the longest x2 10.7 us: on_device(): flat = flat + jnp.swapaxes(jnp.take(two[0], stored, axis=0), 0, 1)]
  transfers between devices with their start and end apart: 4 -> 7, of which waited for: 4 -> 4; matrix products, arithmetic and copies ran while one was open for 3% -> 51% of each run, Pallas kernels for 0% -> 0%
where the time goes in v1:
time: 788 us; the launch traced here: 778 us
  local copies, waits for them, and re-layouts  357 us (45%)
  waiting for transfers between devices  242 us (31%)
  other arithmetic  86.2 us (11%)
  matrix products  35.2 us (4%)
  starting transfers between devices  31.8 us (4%)
  between operations  14.4 us (2%)
  blocking collectives  11 us (1%)
    unnamed x14, local copies, waits for them, and re-layouts  217 us
    all_to_all x1, waiting for transfers between devices, on_device(): lax.all_to_all(slope_z, 'col', split_axis=0, concat_axis=2, tiled=True)  88.7 us
    all_to_all x2, waiting for transfers between devices, col_exchange(): lax.all_to_all(value, 'col', split_axis=split, concat_axis=concat, tiled=...  81.3 us
    pmax x1, waiting for transfers between devices, on_device(): peak = lax.pmax(local_peak, 'col')  54.4 us
    all_to_all x5, local copies, waits for them, and re-layouts, row_exchange(): lax.all_to_all(value, 'row', split_axis=split, concat_axis=concat, tiled=...  48 us
    all_to_all x2, other arithmetic, row_exchange(): lax.all_to_all(value, 'row', split_axis=split, concat_axis=concat, tiled=...  47.6 us
    another operation x1, local copies, waits for them, and re-layouts, on_device(): along_y = jnp.stack([slope_x, velocity[1]])  27.3 us
    all_to_all x3, waiting for transfers between devices, row_exchange(): lax.all_to_all(value, 'row', split_axis=split, concat_axis=concat, tiled=...  17.6 us
  transfers between devices with their start and end apart: 7, of which 4 were waited for; matrix products, arithmetic and copies ran while one was open for 51% of the time, Pallas kernels for 0%

profile of v1, /device:TPU:0, one launch (start us, length us, event | category | flops | bytes accessed | tf_op | source)
XLA Modules:
  0.0 778.0 jit_solution(7292383737118666596)
XLA Ops:
  7.2 11.7 %fusion.149 = (f32[1,1,2,36,32,512]{5,4,3,2,1,0:T(8,128)}, f32[1,1,2,36,32,512]{5,4,3,2,1,0:T(8,128)}, f32[1,1,2,36,32,512]{5,4,3,2,1,0:T(8,128)}) fusion(f32[3,1,2,36,32,512]{5,4,3,2,1,0:T(8,128)} %param.10), kind=kLoop, calls=%fused_computation.195 | loop fusion | bytes 28311552 | tf_op jit(solution)/shard_map/slice | solution.py:67
  18.9 14.8 %copy.99 = f32[1,1,2,36,32,512]{3,4,2,5,1,0:T(8,128)} copy(f32[1,1,2,36,32,512]{5,4,3,2,1,0:T(8,128)} %get-tuple-element.28) | data formatting | bytes 9437184
  33.7 12.2 %bitcast_bitcast_fusion = f32[512,2,32,36]{3,2,1,0:T(8,128)} fusion(f32[1,1,2,36,32,512]{3,4,2,5,1,0:T(8,128)} %copy.99), kind=kLoop, calls=%fused_computation.199 | loop fusion | bytes 9437184
  45.9 25.2 %reshape.277 = f32[4,1,294912]{2,1,0:T(1,128)} reshape(f32[512,2,32,36]{3,2,1,0:T(8,128)} %bitcast_bitcast_fusion) | data formatting | bytes 9437184
  71.1 5.6 all-to-all-start.2
  81.8 12.6 %fusion.6 = f32[1,2,36,32,512]{4,2,3,1,0:T(8,128)S(1)} fusion(f32[1,1,2,36,32,512]{5,4,3,2,1,0:T(8,128)} %get-tuple-element.29), kind=kOutput, calls=%fused_computation.15 | convolution fusion | flops 3632791552 | bytes 9437184 | tf_op jit(solution)/shard_map/dot_general | solution.py:64
  94.4 5.5 pad_maximum_fusion
  99.9 27.3 %copy.76 = f32[2,2,36,32,512]{2,3,1,0,4:T(8,128)} copy(f32[2,2,36,32,512]{4,2,3,1,0:T(8,128)} %pad_maximum_fusion) | data formatting | bytes 18874368 | tf_op jit(solution)/shard_map/stack | solution.py:65
  127.2 63.4 %reshape.275 = f32[4,1,589824]{2,1,0:T(1,128)} reshape(f32[512,2,2,32,36]{4,3,2,1,0:T(8,128)} %bitcast.94) | data formatting | bytes 18874368
  190.6 5.9 all-to-all-start
  198.9 10.2 %compare_and_fusion = (pred[256]{0:T(512)(128)(4,1)S(1)}, s32[256]{0:T(256)S(1)}) fusion(s32[]{:T(128)} %bitcast.28, s32[]{:T(128)} %bitcast.27, s32[]{:T(128)} %bitcast.26, s32[]{:T(128)} %bitcast.25, s32[]{:T(128)} %bitcast.24, s32[]{:T(128)} %bitcast.23, s32[]{:T(128)} %bitcast.22, s32[]{:T(128)} %bitcast.21, s32[]{:T(128)} %bitcast.20, s32[]{:T(128)} %bitcast.19, ...), kind=kLoop, calls=%fused_computation.152 | loop fusion | flops 9728 | bytes 2368 | tf_op jit(solution)/shard_map/jit(_take)/and | solution.py:86
  209.6 17.3 %reduce.2 = f32[4,294912]{1,0:T(4,128)} reduce(f32[4,1,294912]{2,1,0:T(1,128)} %all-to-all-done.2, f32[]{:T(128)} %broadcast.303), dimensions={1}, to_apply=%all_to_all.54.reduce_sub_computation | reduce | bytes 9437188 | tf_op jit(solution)/shard_map/all_to_all | solution.py:32
  227.0 30.3 %reshape.278 = f32[512,2,32,36]{3,2,1,0:T(8,128)} reshape(f32[4,294912]{1,0:T(4,128)} %reduce.2) | data formatting | bytes 9437184
  257.3 12.3 %copy.96 = f32[2,36,32,4,128]{4,3,2,1,0:T(4,128)} copy(f32[2,36,32,4,128]{1,2,0,4,3:T(8,128)} %bitcast.96) | data formatting | bytes 9437184 | tf_op jit(solution)/shard_map/all_to_all | solution.py:32
  283.8 17.6 %all-to-all-done = f32[4,1,589824]{2,1,0:T(1,128)} async-done(((f32[4,1,589824]{2,1,0:T(1,128)}), f32[4,1,589824]{2,1,0:T(1,128)}, u32[]{:S(2)}, u32[]{:S(2)}) %all-to-all-start) | async-done | bytes 9437216 | tf_op jit(solution)/shard_map/all_to_all | solution.py:32
  307.0 30.3 %reduce.1 = f32[4,589824]{1,0:T(4,128)} reduce(f32[4,1,589824]{2,1,0:T(1,128)} %all-to-all-done, f32[]{:T(128)} %broadcast.303), dimensions={1}, to_apply=%all_to_all.50.reduce_sub_computation | reduce | bytes 18874372 | tf_op jit(solution)/shard_map/all_to_all | solution.py:32
  337.3 64.9 %reshape.276 = f32[512,2,2,32,36]{4,3,2,1,0:T(8,128)} reshape(f32[4,589824]{1,0:T(4,128)} %reduce.1) | data formatting | bytes 18874368
  402.2 23.3 %copy.95 = f32[2,2,36,32,4,128]{5,4,3,2,1,0:T(4,128)} copy(f32[2,2,36,32,4,128]{2,3,1,0,5,4:T(8,128)} %bitcast.95) | data formatting | bytes 18874368 | tf_op jit(solution)/shard_map/all_to_all | solution.py:32
  425.5 8.6 %fusion.150 = (f32[1,4,2,36,32,128]{5,1,4,3,2,0:T(4,128)}, f32[1,4,2,36,32,128]{5,1,4,3,2,0:T(4,128)S(1)}) fusion(f32[2,4,2,36,32,128]{5,1,4,3,2,0:T(4,128)} %bitcast.97), kind=kLoop, calls=%fused_computation.196 | loop fusion | bytes 18874368 | tf_op jit(solution)/shard_map/slice | solution.py:85
  442.1 5.5 copy.81
  451.2 10.1 %bitcast_add_fusion.1 = f32[32,256,128]{1,2,0:T(8,128)} fusion(f32[256,32,128]{0,2,1:T(8,128)S(1)} %copy-done, f32[288,32,128]{2,1,0:T(8,128)S(1)} %bitcast.99, pred[256]{0:T(512)(128)(4,1)S(1)} %get-tuple-element.26, f32[288]{0:T(512)S(1)} %get-tuple-element.23, s32[288]{0:T(512)S(1)} %convert_element_type.48), kind=kOutput, calls=%fused_computation.12 | convolution fusion | flops 1816616960 | bytes 13109760 | tf_op jit(solution)/shard_map/jy,yzx->zjx/dot_general | solution.py:85
  471.1 5.6 all-to-all-start.1
  476.8 12.5 %fusion.7 = f32[8,32,32,128]{3,1,2,0:T(8,128)} fusion(f32[8,32,32,128]{3,2,1,0:T(8,128)} %all-to-all-done.3, s32[8,32]{1,0:T(8,128)S(1)} %multiply_add_fusion, s32[8,32]{1,0:T(8,128)S(1)} %copy.83), kind=kOutput, calls=%fused_computation.16 | convolution fusion | flops 1612840960 | bytes 8390656 | tf_op jit(solution)/shard_map/akz,kyzx->ayx/dot_general | solution.py:75
  489.3 81.3 %all-to-all-done.1 = f32[8,4,256,128]{2,3,1,0:T(8,128)} async-done(((f32[8,4,256,128]{2,3,1,0:T(8,128)}), f32[8,4,256,128]{2,3,1,0:T(8,128)}, u32[]{:S(2)}, u32[]{:S(2)}) %all-to-all-start.1) | async-done | bytes 4194336 | tf_op jit(solution)/shard_map/all_to_all | solution.py:36
  575.2 5.3 copy.82
  580.6 88.7 %all-to-all-done.4 = f32[8,32,32,128]{3,1,2,0:T(8,128)} async-done(((f32[8,32,32,128]{3,1,2,0:T(8,128)}), f32[8,32,32,128]{3,1,2,0:T(8,128)}, u32[]{:S(2)}, u32[]{:S(2)}) %all-to-all-start.4) | async-done | bytes 4194336 | tf_op jit(solution)/shard_map/all_to_all | solution.py:82
  669.2 7.9 %bitcast_add_fusion = f32[32,256,128]{2,1,0:T(8,128)} fusion(f32[8,4,256,128]{3,2,1,0:T(8,128)} %copy.82, f32[32,256,128]{2,0,1:T(8,128)} %bitcast.49), kind=kLoop, calls=%fused_computation.11 | loop fusion | flops 1048576 | bytes 12582912 | tf_op jit(solution)/shard_map/add | solution.py:90
  682.0 5.5 copy.90
  692.2 54.4 %all-reduce.2.cloned.1.call-done = f32[256,128]{0,1:T(8,128)} async-done(((f32[256,128]{0,1:T(8,128)}), f32[256,128]{0,1:T(8,128)}) %all-reduce.2.cloned.1.call-update) | async-done | bytes 131088 | tf_op jit(solution)/shard_map/pmax | solution.py:92
  746.7 11.0 %all_gather.3 = f32[256,512]{0,1:T(8,128)S(1)} all-gather(f32[256,128]{0,1:T(8,128)} %all-reduce.2.cloned.1.call-done), channel_id=1, replica_groups=mesh['row'=4,'col'=8] {'row'}, dimensions={1}, use_global_device_ids=true | all-gather | bytes 655360 | tf_op jit(solution)/shard_map/all_gather | solution.py:93
  758.7 6.8 copy.89
  765.5 5.5 reshape.144
  (45 shorter events, 64.5 us)
Async XLA Ops:
  71.1 119.5 %all-to-all-start.2 = ((f32[4,1,294912]{2,1,0:T(1,128)}), f32[4,1,294912]{2,1,0:T(1,128)}, u32[]{:S(2)}, u32[]{:S(2)}) async-start(f32[4,1,294912]{2,1,0:T(1,128)} %reshape.277), calls=%async_computation.2 | async-start | bytes 9437184 | tf_op jit(solution)/shard_map/all_to_all | solution.py:32
  190.6 6.0 copy-start.2
  190.6 110.8 %all-to-all-start = ((f32[4,1,589824]{2,1,0:T(1,128)}), f32[4,1,589824]{2,1,0:T(1,128)}, u32[]{:S(2)}, u32[]{:S(2)}) async-start(f32[4,1,589824]{2,1,0:T(1,128)} %reshape.275), calls=%async_computation | async-start | bytes 18874368 | tf_op jit(solution)/shard_map/all_to_all | solution.py:32
  301.4 5.4 copy-start.1
  301.4 169.6 %all-to-all-start.3 = ((f32[8,32,32,128]{3,2,1,0:T(8,128)}), f32[8,32,32,128]{3,2,1,0:T(8,128)}, u32[]{:S(2)}, u32[]{:S(2)}) async-start(f32[8,32,32,128]{3,2,1,0:T(8,128)} %bitcast.104), calls=%async_computation.3 | async-start | bytes 8388608 | tf_op jit(solution)/shard_map/all_to_all | solution.py:36
  447.6 3.6 copy-start
  471.1 99.6 %all-to-all-start.1 = ((f32[8,4,256,128]{2,3,1,0:T(8,128)}), f32[8,4,256,128]{2,3,1,0:T(8,128)}, u32[]{:S(2)}, u32[]{:S(2)}) async-start(f32[8,4,256,128]{2,3,1,0:T(8,128)} %broadcast_select_fusion.1), calls=%async_computation.1 | async-start | bytes 8388608 | tf_op jit(solution)/shard_map/all_to_all | solution.py:36
  570.7 98.6 %all-to-all-start.4 = ((f32[8,32,32,128]{3,1,2,0:T(8,128)}), f32[8,32,32,128]{3,1,2,0:T(8,128)}, u32[]{:S(2)}, u32[]{:S(2)}) async-start(f32[8,32,32,128]{3,1,2,0:T(8,128)} %fusion.7), calls=%async_computation.4 | async-start | bytes 8388608 | tf_op jit(solution)/shard_map/all_to_all | solution.py:82
  677.1 81.5 %all-to-all-start.5 = ((f32[32,256,128]{2,1,0:T(8,128)}), f32[32,256,128]{2,1,0:T(8,128)}, u32[]{:S(2)}, u32[]{:S(2)}) async-start(f32[32,256,128]{2,1,0:T(8,128)} %bitcast_add_fusion), calls=%async_computation.5 | async-start | bytes 8388608 | tf_op jit(solution)/shard_map/all_to_all | solution.py:32
  682.0 64.7 %all-reduce.2.cloned.1.call-start = ((), (), s32[]{:S(2)}) async-start(), calls=%async_computation.6 | async-start | bytes 262144 | tf_op jit(solution)/shard_map/pmax | solution.py:92
Sparse Core Ops, SparseCore 0:
  692.4 54.2 all-reduce.1

commit v2 on v1

--- a/solution.py
+++ b/solution.py
@@ -1,14 +1,90 @@
+import functools
 import math
 
 import jax
 import jax.numpy as jnp
 from jax import lax
+from jax.experimental import pallas as pl
+from jax.experimental.pallas import tpu as pltpu
 from jax.sharding import PartitionSpec as P
 
 YMEAN = 32
 
 
 FINE = lax.Precision.HIGH
+
+LANES = 128
+
+
+def exchange_kernel(jobs, sizes, count_in, count_out, *refs):
+    ins, outs = refs[:count_in], refs[count_in : count_in + count_out]
+    rest = refs[count_in + count_out :]
+    held, (send_sem, recv_sem, in_sem, out_sem) = rest[: len(jobs)], rest[len(jobs) :]
+    barrier = pltpu.get_barrier_semaphore()
+    greeted = 0
+    for axis in sorted({job[2] for job in jobs}):
+        me = lax.axis_index(axis)
+        for step in range(1, sizes[axis]):
+            partner = lax.rem(me + step, sizes[axis])
+            pl.semaphore_signal(
+                barrier, inc=1, device_id={axis: partner}, device_id_type=pl.DeviceIdType.MESH
+            )
+            greeted += 1
+    pl.semaphore_wait(barrier, greeted)
+    copies, own = [], []
+    at = 0
+    for number, (source, target, axis, pick, put) in enumerate(jobs):
+        size = sizes[axis]
+        me = lax.axis_index(axis)
+        for step in range(1, size):
+            partner = lax.rem(me + step, size)
+            copy = pltpu.make_async_remote_copy(
+                src_ref=pick(ins[source], partner),
+                dst_ref=put(outs[target], me),
+                send_sem=send_sem.at[at],
+                recv_sem=recv_sem.at[at],
+                device_id={axis: partner},
+                device_id_type=pl.DeviceIdType.MESH,
+            )
+            copy.start()
+            copies.append(copy)
+            at += 1
+    for number, (source, target, axis, pick, put) in enumerate(jobs):
+        me = lax.axis_index(axis)
+        copy = pltpu.make_async_copy(pick(ins[source], me), held[number], in_sem.at[number])
+        copy.start()
+        own.append(copy)
+    last = []
+    for number, (source, target, axis, pick, put) in enumerate(jobs):
+        me = lax.axis_index(axis)
+        own[number].wait()
+        copy = pltpu.make_async_copy(held[number], put(outs[target], me), out_sem.at[number])
+        copy.start()
+        last.append(copy)
+    for copy in last:
+        copy.wait()
+    for copy in copies:
+        copy.wait()
+
+
+def exchange(number, inputs, outputs, jobs, blocks):
+    sizes = {axis: lax.axis_size(axis) for axis in ("row", "col")}
+    total = sum(sizes[job[2]] - 1 for job in jobs)
+    dma = pltpu.SemaphoreType.DMA
+    return pl.pallas_call(
+        functools.partial(exchange_kernel, jobs, sizes, len(inputs), len(outputs)),
+        out_shape=[jax.ShapeDtypeStruct(shape, jnp.float32) for shape in outputs],
+        in_specs=[pl.BlockSpec(memory_space=pl.ANY)] * len(inputs),
+        out_specs=[pl.BlockSpec(memory_space=pl.ANY)] * len(outputs),
+        scratch_shapes=[pltpu.VMEM(block, jnp.float32) for block in blocks]
+        + [dma((total,)), dma((total,)), dma((len(jobs),)), dma((len(jobs),))],
+        compiler_params=pltpu.CompilerParams(collective_id=number, has_side_effects=True),
+        name=f"exchange{number}",
+    )(*inputs)
+
+
+def lanes(part):
+    return pl.ds(pl.multiple_of(part * LANES, LANES), LANES)
 
 
 def spectral_matrix(to, source, count):
@@ -37,6 +113,7 @@
 
 
 def on_device(velocity, y_sizes, old_place, new_col):
+    saved = velocity
     velocity = velocity[:, 0]
     fields, places, row_depth, planes, x_cells = velocity.shape
     columns = lax.axis_size("col")
@@ -62,13 +139,43 @@
     across_x = spectral_matrix(steps_x, steps_x, x_cells)
 
     slope_x = jnp.dot(velocity[0], across_x.T, precision=FINE, preferred_element_type=jnp.float32)
-    along_y = jnp.stack([slope_x, velocity[1]])
-    two = row_exchange(along_y, 4, 1)
-    third = row_exchange(velocity[2], 3, 0)
-    two = two.reshape(2, blocks_y * row_depth, planes, x_part)
+    direct = x_part == LANES
+    parted = (rows_count, places, row_depth, planes, x_part)
+    pencil = parted[1:]
+    slab = (columns, y_part, planes, x_part)
+    whole = lambda ref, part: ref
+    nth = lambda ref, part: ref.at[part]
+    if direct:
+        (third,) = exchange(
+            0,
+            [saved],
+            [parted],
+            [(0, 0, "row", lambda ref, part: ref.at[2, 0, :, :, :, lanes(part)], nth)],
+            [pencil],
+        )
+    else:
+        along_y = jnp.stack([slope_x, velocity[1]])
+        two = row_exchange(along_y, 4, 1)
+        third = row_exchange(velocity[2], 3, 0)
     third = third.reshape(blocks_y * row_depth, planes, x_part)
     upright = jnp.take(third, stored, axis=0)
-    upright = col_exchange(upright.reshape(columns, y_part, planes, x_part), 0, 0)
+    upright = upright.reshape(slab)
+    if direct:
+        first_part, second_part, upright = exchange(
+            1,
+            [upright, slope_x, saved],
+            [parted, parted, slab],
+            [
+                (0, 2, "col", nth, nth),
+                (1, 0, "row", lambda ref, part: ref.at[:, :, :, lanes(part)], nth),
+                (2, 1, "row", lambda ref, part: ref.at[1, 0, :, :, :, lanes(part)], nth),
+            ],
+            [slab[1:], pencil, pencil],
+        )
+        two = [first_part, second_part]
+    else:
+        upright = col_exchange(upright, 0, 0)
+    two = [one.reshape(blocks_y * row_depth, planes, x_part) for one in two]
     first = slots[None, :, None] * planes + slab_of.T[:, :, None] * thick
     targets = (first + jnp.arange(thick, dtype=jnp.int32)).reshape(-1)
     across_z = spectral_matrix(targets, jnp.arange(depth, dtype=jnp.int32), depth)
@@ -79,20 +186,51 @@
         precision=FINE,
     )
     slope_z = slope_z.reshape(columns, planes, y_part, x_part)
-    slope_z = lax.all_to_all(
-        slope_z, "col", split_axis=0, concat_axis=2, tiled=True
-    ).reshape(planes, height, x_part)
     flat = jnp.einsum("jy,yzx->zjx", across_y, two[1], precision=FINE)
     flat = flat + jnp.swapaxes(jnp.take(two[0], stored, axis=0), 0, 1)
     flat = flat.reshape(columns, thick, height, x_part)
     flat = jnp.take(flat, jnp.take(slab_of, my_col, axis=0), axis=0)
-    flat = col_exchange(flat, 0, 0).reshape(planes, height, x_part)
+    if direct:
+        flat, slope_z = exchange(
+            2,
+            [flat, slope_z],
+            [(columns, thick, height, x_part), (planes, height, x_part)],
+            [
+                (0, 0, "col", nth, nth),
+                (1, 1, "col", nth, lambda ref, part: ref.at[:, pl.ds(part * y_part, y_part), :]),
+            ],
+            [(thick, height, x_part), (planes, y_part, x_part)],
+        )
+        flat = flat.reshape(planes, height, x_part)
+    else:
+        flat = col_exchange(flat, 0, 0).reshape(planes, height, x_part)
+        slope_z = col_exchange(slope_z, 0, 2).reshape(planes, height, x_part)
     part = flat + slope_z
     local_peak = jnp.max(jnp.abs(part), axis=0)
-    peak = lax.pmax(local_peak, "col")
-    peak = lax.all_gather(peak, "row", axis=1, tiled=True)
-    field = row_exchange(part, 0, 2)
-    field = field.reshape(columns // rows_count, 1, thick, height, x_cells)
+    per_row = columns // rows_count
+    if direct:
+        field, peaks = exchange(
+            3,
+            [part.reshape(rows_count, per_row, thick, height, x_part), local_peak],
+            [(per_row, 1, thick, height, x_cells), (columns, height, x_part)],
+            [
+                (0, 0, "row", nth, lambda ref, part: ref.at[:, 0, :, :, lanes(part)]),
+                (1, 1, "col", whole, nth),
+            ],
+            [(per_row, thick, height, x_part), (height, x_part)],
+        )
+        (peak,) = exchange(
+            4,
+            [jnp.max(peaks, axis=0)],
+            [(height, x_cells)],
+            [(0, 0, "row", whole, lambda ref, part: ref.at[:, lanes(part)])],
+            [(height, x_part)],
+        )
+    else:
+        peak = lax.pmax(local_peak, "col")
+        peak = lax.all_gather(peak, "row", axis=1, tiled=True)
+        field = row_exchange(part, 0, 2)
+        field = field.reshape(per_row, 1, thick, height, x_cells)
     return (field, peak)
 
 

time: 788 us -> 512 us (0.65); the launches traced: 778 us -> 511 us
  Pallas kernels: 0 us -> 406 us
  local copies, waits for them, and re-layouts: 357 us -> 37.3 us
  waiting for transfers between devices: 242 us -> 0 us
  other arithmetic: 86.2 us -> 30.1 us
  starting transfers between devices: 31.8 us -> 0 us
  between operations: 14.4 us -> 0.75 us
  blocking collectives: 11 us -> 0 us
    pallas_call x0 -> x5, Pallas kernels: none -> 406 us  [exchange(): pl.pallas_call(functools.partial(exchange_kernel, jobs, sizes, len(inputs...]
    unnamed x14 -> x6, local copies, waits for them, and re-layouts: 217 us -> 5.5 us
    all_to_all x6 -> x0, waiting for transfers between devices: 188 us -> none  [the longest x1 88.7 us: on_device(): lax.all_to_all(slope_z, 'col', split_axis=0, concat_axis=2, tiled=True)]
    pmax x1 -> x0, waiting for transfers between devices: 54.4 us -> none  [on_device(): peak = lax.pmax(local_peak, 'col')]
    all_to_all x6 -> x0, local copies, waits for them, and re-layouts: 53.3 us -> none  [the longest x5 48 us: row_exchange(): lax.all_to_all(value, 'row', split_axis=split, concat_axis=concat, tiled=...]
    all_to_all x2 -> x0, other arithmetic: 47.6 us -> none  [row_exchange(): lax.all_to_all(value, 'row', split_axis=split, concat_axis=concat, tiled=...]
    all_to_all x6 -> x0, starting transfers between devices: 31.8 us -> none  [the longest x3 16.4 us: row_exchange(): lax.all_to_all(value, 'row', split_axis=split, concat_axis=concat, tiled=...]
    another operation x1 -> x0, local copies, waits for them, and re-layouts: 27.3 us -> none  [on_device(): along_y = jnp.stack([slope_x, velocity[1]])]
  transfers between devices with their start and end apart: 7 -> 0, of which waited for: 4 -> 0; matrix products, arithmetic and copies ran while one was open for 51% -> 0% of each run, Pallas kernels for 0% -> 0%
where the time goes in v2:
time: 512 us; the launch traced here: 511 us
  Pallas kernels  406 us (79%)
  local copies, waits for them, and re-layouts  37.3 us (7%)
  matrix products  37 us (7%)
  other arithmetic  30.1 us (6%)
    pallas_call x5, Pallas kernels, exchange(): pl.pallas_call(functools.partial(exchange_kernel, jobs, sizes, len(inputs...  406 us
    dot_general x1, matrix products, on_device(): flat = jnp.einsum('jy,yzx->zjx', across_y, two[1], precision=FINE)  13.6 us
    dot_general x1, matrix products, on_device(): jnp.dot(velocity[0], across_x.T, precision=FINE, preferred_element_type=j...  12.8 us
    dot_general x1, matrix products, on_device(): jnp.einsum('akz,kyzx->ayx', across_z.reshape(depth, columns, planes), upr...  10.6 us
    gather x2, local copies, waits for them, and re-layouts, on_device(): flat = flat + jnp.swapaxes(jnp.take(two[0], stored, axis=0), 0, 1)  10.5 us

profile of v2, /device:TPU:0, one launch (start us, length us, event | category | flops | bytes accessed | tf_op | source)
XLA Modules:
  0.0 511.0 jit_solution(17090319086062320679)
XLA Ops:
  0.6 0.7 fusion.122
  1.3 0.7 fusion.153
  2.0 0.8 reduce-window.8
  2.8 0.7 bitcast_subtract_fusion
  3.5 0.7 fusion.154
  4.2 0.1 convert_reduce_fusion.1
  4.3 10.0 %compare_and_fusion = (pred[256]{0:T(512)(128)(4,1)S(1)}, s32[256]{0:T(256)S(1)}) fusion(s32[]{:T(128)} %bitcast.19, s32[]{:T(128)} %bitcast.18, s32[]{:T(128)} %bitcast.17, s32[]{:T(128)} %bitcast.16, s32[]{:T(128)} %bitcast.15, s32[]{:T(128)} %bitcast.14, s32[]{:T(128)} %bitcast.13, s32[]{:T(128)} %bitcast.12, s32[]{:T(128)} %bitcast.11, s32[]{:T(128)} %bitcast.10, ...), kind=kLoop, calls=%fused_computation.151 | loop fusion | flops 9728 | bytes 2368 | tf_op jit(solution)/shard_map/jit(_take)/and | solution.py:161
  14.3 55.9 %exchange0.1 = f32[4,2,36,32,128]{4,3,2,1,0:T(8,128)} custom-call(f32[3,1,2,36,32,512]{5,4,3,2,1,0:T(8,128)} %refs_2_.1), custom_call_target="tpu_custom_call" | custom-call | tf_op jit(solution)/shard_map/exchange0/pallas_call | solution.py:74
  70.3 5.2 %gather_fusion.1 = f32[256,32,128]{2,1,0:T(8,128)} fusion(f32[288,32,128]{2,1,0:T(8,128)} %bitcast.70, s32[1024]{0:T(1024)S(1)} %pad_clamp_fusion.1), kind=kCustom, calls=%fused_computation.clone | custom fusion | bytes 8389632 | tf_op jit(solution)/shard_map/jit(_take)/gather | solution.py:161
  75.4 4.1 broadcast_select_fusion
  79.5 12.8 %fusion.8.refs_1_ = f32[2,36,32,512]{3,2,1,0:T(8,128)} fusion(f32[3,1,2,36,32,512]{5,4,3,2,1,0:T(8,128)} %refs_2_.1), kind=kOutput, calls=%fused_computation.14 | convolution fusion | flops 3632791552 | bytes 9437184 | tf_op jit(solution)/shard_map/dot_general | solution.py:141
  92.3 107.8 %exchange1.1 = (f32[4,2,36,32,128]{4,3,2,1,0:T(8,128)}, f32[4,2,36,32,128]{4,3,2,1,0:T(8,128)}, f32[8,32,32,128]{3,2,1,0:T(8,128)}) custom-call(f32[8,32,32,128]{3,2,1,0:T(8,128)} %bitcast.73, f32[2,36,32,512]{3,2,1,0:T(8,128)} %fusion.8.refs_1_, f32[3,1,2,36,32,512]{5,4,3,2,1,0:T(8,128)} %refs_2_.1), custom_call_target="tpu_custom_call" | custom-call | tf_op jit(solution)/shard_map/exchange1/pallas_call | solution.py:74
  200.1 5.2 %gather_fusion.2 = f32[256,32,128]{2,1,0:T(8,128)} fusion(f32[288,32,128]{2,1,0:T(8,128)} %bitcast.75, s32[1024]{0:T(1024)S(1)} %pad_clamp_fusion.1), kind=kCustom, calls=%fused_computation.1.clone | custom fusion | bytes 8389632 | tf_op jit(solution)/shard_map/jit(_take)/gather | solution.py:190
  205.3 5.4 %copy.21 = f32[256,32,128]{0,2,1:T(8,128)} copy(f32[256,32,128]{2,1,0:T(8,128)} %gather_fusion.2) | data formatting | bytes 8388608 | tf_op jit(solution)/shard_map/jit(_take)/gather | solution.py:190
  210.6 0.2 select_reduce_fusion
  210.8 13.6 %bitcast_add_fusion.1 = f32[32,256,128]{1,2,0:T(8,128)} fusion(f32[256,32,128]{0,2,1:T(8,128)} %copy.21, f32[288,32,128]{2,1,0:T(8,128)} %bitcast.74, pred[256]{0:T(512)(128)(4,1)S(1)} %get-tuple-element.36, f32[288]{0:T(512)S(1)} %get-tuple-element.31, s32[288]{0:T(512)S(1)} %convert_element_type.48), kind=kOutput, calls=%fused_computation.11 | convolution fusion | flops 1816616960 | bytes 13109760 | tf_op jit(solution)/shard_map/jy,yzx->zjx/dot_general | solution.py:189
  224.5 5.3 %copy.22 = f32[8,4,256,128]{3,2,1,0:T(8,128)} copy(f32[8,4,256,128]{2,3,1,0:T(8,128)} %bitcast.72) | data formatting | bytes 8388608 | tf_op jit(solution)/shard_map/reshape | solution.py:191
  229.8 0.0 copy-done.1
  229.8 0.1 select_reduce_fusion.1
  229.9 5.0 gather_fusion
  234.9 4.9 broadcast_select_fusion.1.refs_0_
  239.8 0.1 add_bitcast_fusion
  239.9 0.1 copy.23
  240.0 10.6 %fusion.11 = f32[8,32,32,128]{3,1,2,0:T(8,128)S(1)} fusion(f32[8,32,32,128]{3,2,1,0:T(8,128)} %get-tuple-element.14, s32[8,32]{1,0:T(8,128)S(1)} %multiply_add_fusion, s32[8,32]{1,0:T(8,128)S(1)} %copy.23), kind=kOutput, calls=%fused_computation.15 | convolution fusion | flops 1612840960 | bytes 8390656 | tf_op jit(solution)/shard_map/akz,kyzx->ayx/dot_general | solution.py:182
  250.5 4.3 copy.25.refs_1_
  254.8 151.2 %exchange2.1 = (f32[8,4,256,128]{3,2,1,0:T(8,128)}, f32[32,256,128]{2,1,0:T(8,128)}) custom-call(f32[8,4,256,128]{3,2,1,0:T(8,128)} %broadcast_select_fusion.1.refs_0_, f32[8,32,32,128]{3,2,1,0:T(8,128)} %copy.25.refs_1_), custom_call_target="tpu_custom_call" | custom-call | tf_op jit(solution)/shard_map/exchange2/pallas_call | solution.py:74
  406.0 6.6 %abs_reduce_fusion = (f32[256,128]{1,0:T(8,128)}, f32[32,256,128]{2,1,0:T(8,128)}) fusion(f32[32,256,128]{2,1,0:T(8,128)} %get-tuple-element.16, f32[8,4,256,128]{3,2,1,0:T(8,128)} %get-tuple-element.15), kind=kLoop, calls=%fused_computation.13 | loop fusion | flops 3112960 | bytes 12713984 | tf_op jit(solution)/shard_map/reduce_max | solution.py:209
  412.6 81.9 %exchange3.1 = (f32[2,1,4,256,512]{4,3,2,1,0:T(8,128)}, f32[8,256,128]{2,1,0:T(8,128)}) custom-call(f32[4,2,4,256,128]{4,3,2,1,0:T(8,128)} %bitcast.71, f32[256,128]{1,0:T(8,128)} %get-tuple-element.32.refs_1_), custom_call_target="tpu_custom_call" | custom-call | tf_op jit(solution)/shard_map/exchange3/pallas_call | solution.py:74
  494.5 1.9 reduce_max.19.refs_0_
  496.4 9.1 %exchange4.1 = f32[256,512]{1,0:T(8,128)} custom-call(f32[256,128]{1,0:T(8,128)} %reduce_max.19.refs_0_), custom_call_target="tpu_custom_call" | custom-call | tf_op jit(solution)/shard_map/exchange4/pallas_call | solution.py:74
  505.5 4.7 copy.41
  510.2 0.8 copy.42
  (12 shorter events, 0.1 us)
Async XLA Ops:
  224.4 5.3 %copy-start.1 = (s32[8,8]{1,0:T(8,128)S(1)}, s32[8,8]{1,0:T(8,128)}, u32[]{:S(2)}) copy-start(s32[8,8]{1,0:T(8,128)} %param.13) | copy-start | bytes 772
  505.5 4.7 copy-start
